TPU v7x, 32 devices: a 4x4x1 block of a 4x4x8 slice. The times are simulated.
32 devices in a mesh: data: 1 (over z), col: 4 (over y), row: 8 (over x, core).
Axes of the slice: x: 4, y: 4, z: 1, core: 2. Of those that a mesh axis runs over, the one named last changes fastest.
The devices are a block of a 4x4x8 slice.
Arguments:
- image: bfloat16 [256, 128, 4], P(('data', 'row'), 'col')
- w_enc1a: bfloat16 [3, 3, 4, 320], replicated
- b_enc1a: float32 [320], replicated
- w_enc1b: bfloat16 [3, 3, 320, 320], replicated
- b_enc1b: float32 [320], replicated
- w_enc2a: bfloat16 [3, 3, 320, 640], replicated
- b_enc2a: float32 [640], replicated
- w_enc2b: bfloat16 [3, 3, 640, 640], replicated
- b_enc2b: float32 [640], replicated
- w_mid_a: bfloat16 [3, 3, 640, 1280], replicated
- b_mid_a: float32 [1280], replicated
- w_mid_b: bfloat16 [3, 3, 1280, 1280], replicated
- b_mid_b: float32 [1280], replicated
- w_up2: bfloat16 [2, 2, 1280, 640], replicated
- w_dec2a: bfloat16 [3, 3, 1280, 640], replicated
- b_dec2a: float32 [640], replicated
- w_dec2b: bfloat16 [3, 3, 640, 640], replicated
- b_dec2b: float32 [640], replicated
- w_up1: bfloat16 [2, 2, 640, 320], replicated
- w_dec1a: bfloat16 [3, 3, 640, 320], replicated
- b_dec1a: float32 [320], replicated
- w_dec1b: bfloat16 [3, 3, 320, 320], replicated
- b_dec1b: float32 [320], replicated
- w_head: bfloat16 [320, 4], replicated
- b_head: float32 [4], replicated
Outputs:
- output: float32 [256, 128, 4], P(('data', 'row'), 'col')
All inputs are finite; a program needn't handle non-finite values.
Results may differ from a plain program's by a relative error of at most 0.0171244.
Values are sent between devices in bfloat16 or wider.
A program may use at most 768 MiB of HBM per device.

v0:
```python
import functools

import jax
import jax.numpy as jnp
from jax import lax
from jax.experimental import pallas as pl
from jax.experimental.pallas import tpu as pltpu
from jax.sharding import PartitionSpec as P

F32 = jnp.float32
BF16 = jnp.bfloat16
LANE = 128
DIRS = ((-1, 0), (1, 0), (0, -1), (0, 1), (-1, -1), (-1, 1), (1, -1), (1, 1))


def lane_tiles(channels):
    return [(t, t * LANE, min(LANE, channels - t * LANE)) for t in range(-(-channels // LANE))]


def mm(lhs, rhs, transposed):
    contract = (((1,), (1 if transposed else 0,)), ((), ()))
    return lax.dot_general(lhs, rhs, contract, preferred_element_type=F32)


class Map:
    def __init__(self, index, height, width, channels, refs, small):
        self.index, self.height, self.width, self.channels = index, height, width, channels
        if not small:
            self.x, self.el, self.er, self.hl, self.hr, self.cs, self.cr = refs
            self.top, self.bottom = self.x.at[1], self.x.at[height]
            self.above, self.below = self.x.at[0], self.x.at[height + 1]
        else:
            self.top, self.bottom, self.above, self.below, self.el, self.er, self.hl, self.hr, self.cs, self.cr = refs

    def copy_refs(self, d):
        return (
            (self.top, self.below), (self.bottom, self.above), (self.el, self.hr), (self.er, self.hl),
            (self.cs.at[0], self.cr.at[3]), (self.cs.at[1], self.cr.at[2]),
            (self.cs.at[2], self.cr.at[1]), (self.cs.at[3], self.cr.at[0]),
        )[d]

    def landing(self, dr, dc):
        if dc == 0:
            return self.above if dr < 0 else self.below
        if dr == 0:
            return self.hl if dc < 0 else self.hr
        return self.cr.at[(dr > 0) * 2 + (dc > 0)]


def map_scratch(height, width, channels, small):
    if small:
        shapes = [(2, width, channels)] * 4 + [(2, height, channels)] * 4 + [(4, 4, channels)] * 2
    else:
        shapes = [(height + 2, width, channels)] + [(height, channels)] * 4 + [(4, 2, channels)] * 2
    return [pltpu.VMEM(shape, BF16) for shape in shapes]


def map_specs(h1, w1, cin0, c1, c2):
    h2, w2 = h1 // 2, w1 // 2
    one, two = (h1, w1, c1, False), (h2, w2, c2, False)
    return [(h1, w1, cin0, False), one, (h2, w2, c1, False), two, (h2 // 2, w2 // 2, c2, True), two, two, two, one, one, one]


def split(cin):
    main = cin // 256 * 256
    return main, cin - main


def packed_lhs(slabs, cin):
    main, rest = split(cin)
    parts = [slab[:, :main] for slab in slabs] if main else []
    return parts + ([jnp.concatenate([slab[:, main:cin] for slab in slabs], axis=1)] if rest else [])


ALL_ROWS = (0, 1, 2)


def packed_rhs(piece, cin, axis, dys):
    main, rest = split(cin)
    parts = [piece(dy, 0, main) for dy in dys] if main else []
    return parts + ([jnp.concatenate([piece(dy, main, cin) for dy in dys], axis=axis)] if rest else [])


class Taps:
    transposed = False

    def __init__(self, buf, cin, cout, first=0, fold=1, rest=None):
        self.buf, self.cin, self.cout, self.first, self.fold, self.packed = buf, cin, cout, first, fold, rest
        self.main, self.rest = split(cout)

    def piece(self, dy, dx, k0, k1, n0, n1):
        tap = self.first + (dy * 3 + dx) * self.fold
        if self.fold > 1:
            return self.buf[pl.ds(tap, self.fold), :, n0:n1].reshape(self.cin, n1 - n0)[k0:k1]
        return self.buf[tap, k0:k1, n0:n1]

    def columns(self, dx, dys=ALL_ROWS):
        return packed_rhs(lambda dy, k0, k1: self.piece(dy, dx, k0, k1, 0, self.main), self.cin, 0, dys)

    def whole(self, dx, dys=ALL_ROWS):
        return packed_rhs(lambda dy, k0, k1: self.piece(dy, dx, k0, k1, 0, self.cout), self.cin, 0, dys)

    def last_columns(self, dys=ALL_ROWS):
        def piece(dy, k0, k1):
            if self.packed is not None:
                return self.packed[dy, k0:k1, :3 * self.rest]
            return jnp.concatenate([self.piece(dy, dx, k0, k1, self.main, self.cout) for dx in range(3)], axis=1)
        return packed_rhs(piece, self.cin, 0, dys)

    def pack(self):
        for dy in range(3):
            for dx in range(3):
                self.packed[dy, :, dx * self.rest:(dx + 1) * self.rest] = self.piece(dy, dx, 0, self.cin, self.main,
                                                                                     self.cout)


class TapsT(Taps):
    transposed = True

    def __init__(self, buf, cin, cout, lanes):
        super().__init__(buf, cin, cout)
        self.lanes = lanes

    def piece(self, dy, dx, k0, k1, n0, n1):
        start = self.lanes[k0 > 0]
        return self.buf[dy * 3 + dx, n0:n1, start:start + k1 - k0]

    def columns(self, dx, dys=ALL_ROWS):
        return packed_rhs(lambda dy, k0, k1: self.piece(dy, dx, k0, k1, 0, self.main), self.cin, 1, dys)

    def whole(self, dx, dys=ALL_ROWS):
        return packed_rhs(lambda dy, k0, k1: self.piece(dy, dx, k0, k1, 0, self.cout), self.cin, 1, dys)

    def last_columns(self, dys=ALL_ROWS):
        def piece(dy, k0, k1):
            return jnp.concatenate([self.piece(dy, dx, k0, k1, self.main, self.cout) for dx in range(3)], axis=0)
        return packed_rhs(piece, self.cin, 1, dys)


class TapsFirst(Taps):
    def __init__(self, stacked, stacked_rest, cin, cout):
        self.stacked, self.stacked_rest, self.cin, self.cout = stacked, stacked_rest, cin, cout
        self.main, self.rest = split(cout)

    def columns(self, dx, dys=ALL_ROWS):
        return [self.stacked[dx, :3 * self.cin, :self.main]]

    def whole(self, dx, dys=ALL_ROWS):
        return [self.stacked[dx, :3 * self.cin, :]]

    def last_columns(self, dys=ALL_ROWS):
        return [self.stacked_rest[:3 * self.cin, :3 * self.rest]]


def dots(lhs, rhs, transposed):
    total = mm(lhs[0], rhs[0], transposed)
    for a, b in zip(lhs[1:], rhs[1:]):
        total = total + mm(a, b, transposed)
    return total


def unet_kernel(cfg, image, w1a, b1a_, w1b, b1b_, w2a, b2a_, w2b, b2b_, wma, bma_, wmb, bmb_, wu2, wd2a, bd2a_, wd2b,
                bd2b_, wu1, wd1a, bd1a_, wd1b, bd1b_, wh, bh, out, *scratch):
    h1, w1, cin0, c1, c2, c3, rows, cols = cfg
    h2, w2, h3, w3 = h1 // 2, w1 // 2, h1 // 4, w1 // 4
    half = c3 // 2
    refs = list(scratch)

    def take(n):
        got = refs[:n]
        del refs[:n]
        return got

    maps = []
    for h, w, c, small in map_specs(h1, w1, cin0, c1, c2):
        maps.append(Map(len(maps), h, w, c, take(len(map_scratch(h, w, c, small))), small))
    mx, ma1, mp1, ma2, mp2, ms2, mu2, md2, ms1, mu1, md1 = maps
    (acc1, acc2, acc_skip, bscr, tscr, sides, f3, x3, x3b, m3, d2buf, buf_a, buf_b, buf_c, buf_d, buf_e, buf_f, rest_a, stacked, stacked_rest,
     buf_1a, b1a, b1b, b2a, b2b, bma, bmb, bd2a, bd2b, bd1a, bd1b, send_sem, recv_sem, load_sem) = refs

    data = lax.axis_index("data")
    my_col = lax.axis_index("col")
    my_row = lax.axis_index("row")

    def has(dr, dc):
        r, c = my_row + dr, my_col + dc
        return (r >= 0) & (r < rows) & (c >= 0) & (c < cols)

    def peer(dr, dc):
        return (data, my_col + dc, my_row + dr)

    biases = ((b1a_, b1a), (b1b_, b1b), (b2a_, b2a), (b2b_, b2b), (bma_, bma), (bmb_, bmb), (bd2a_, bd2a), (bd2b_, bd2b),
              (bd1a_, bd1a), (bd1b_, bd1b))
    loads = {
        "1a": (w1a, buf_1a),
        "1b": (w1b, buf_a),
        "2a": (w2a, buf_b),
        "2b": (w2b, buf_c),
        "ma0": (wma.at[:, :, :half], buf_d.at[:9]),
        "ma1": (wma.at[:, :, half:c3], buf_d.at[9:18]),
        "mb0": (wmb.at[:, :, :half], buf_e),
        "mb1": (wmb.at[:9, :, half:c3], buf_d.at[:9]),
        "mb2": (wmb.at[9:18, :, half:c3], buf_d.at[9:18]),
        "u2": (wu2, buf_c.at[:8]),
        "d2s": (wd2a.at[:, c2:2 * c2, :], buf_f),
        "d2u": (wd2a.at[:, :c2, :], buf_e.at[:9]),
        "d2b": (wd2b, buf_d.at[:9]),
        "u1": (wu1, buf_d.at[9:11]),
        "d1a": (wd1a, buf_b),
        "d1b": (wd1b, buf_a),
    }
    for i, pair in enumerate(biases):
        loads[i] = pair
    order = list(loads)

    def load(name):
        src, dst = loads[name]
        return pltpu.make_async_copy(src, dst, load_sem.at[order.index(name)])

    def remote(m, d):
        src, dst = m.copy_refs(d)
        return pltpu.make_async_remote_copy(src_ref=src, dst_ref=dst, send_sem=send_sem.at[m.index, d],
                                            recv_sem=recv_sem.at[m.index, d], device_id=peer(*DIRS[d]),
                                            device_id_type=pl.DeviceIdType.MESH)

    def send(m):
        for d in range(8):
            @pl.when(has(*DIRS[d]))
            def _(d=d):
                remote(m, d).start()

    def receive(m, which):
        for d in which:
            @pl.when(has(-DIRS[d][0], -DIRS[d][1]))
            def _(d=d):
                remote(m, d).wait_recv()

    ROWS, COLS = range(2), range(2, 8)

    load("1a").start()
    for i in range(len(biases)):
        load(i).start()
    load("1b").start()
    load("2a").start()
    load("2b").start()

    barrier = pltpu.get_barrier_semaphore()
    for dr, dc in DIRS:
        @pl.when(has(dr, dc))
        def _(dr=dr, dc=dc):
            pl.semaphore_signal(barrier, inc=1, device_id=peer(dr, dc), device_id_type=pl.DeviceIdType.MESH)

    def put_edges(m, acc, lanes=None):
        for t, lo, n in lane_tiles(m.channels):
            tile = acc.at[t]
            left = tile[pl.ds(0, m.height, stride=m.width), :]
            right = tile[pl.ds(m.width - 1, m.height, stride=m.width), :]
            put_columns(m, slice(0, m.height), left, right, (lanes or in_order)(t, lo, n))
            ends = (left[:1], right[:1], left[m.height - 1:], right[m.height - 1:])
            put_corners(m, ends, (lanes or in_order)(t, lo, n))

    def in_order(t, lo, n):
        return [(0, n, lo)]

    def rest_last(t, lo, n):
        rest = split(c1)[1]
        if t == 0:
            return [(rest, n, 0), (0, rest, c1 - rest)]
        return [(0, n, lo - rest)]

    def put_columns(m, rows_, left, right, lanes):
        for a, b, to in lanes:
            m.el[rows_, to:to + b - a] = left[:, a:b].astype(BF16)
            m.er[rows_, to:to + b - a] = right[:, a:b].astype(BF16)

    def put_corners(m, ends, lanes):
        for a, b, to in lanes:
            for k, pixel in enumerate(ends):
                m.cs[k, :, to:to + b - a] = jnp.broadcast_to(pixel[:, a:b], (2, b - a)).astype(BF16)

    def halo_slabs(m, side):
        h, cin = m.height, m.channels
        tscr[8:8 + h, :cin] = (m.hr if side else m.hl)[...].astype(F32)
        tscr[7:8, :cin] = m.cr[side].astype(F32)[:1]
        tscr[8 + h:9 + h, :cin] = m.cr[2 + side].astype(F32)[:1]
        return [tscr[7 + dy:7 + dy + h, :cin].astype(BF16) for dy in range(3)]

    def combine(px, w, cout, put):
        main, rest = split(cout)
        col = lax.broadcasted_iota(jnp.int32, (px, 1), 0) % w

        def shifted(left, right):
            return (jnp.where(col == 0, 0.0, pltpu.roll(left, 1, 0))
                    + jnp.where(col == w - 1, 0.0, pltpu.roll(right, px - 1, 0)))

        for t in range(main // LANE):
            lanes = slice(t * LANE, (t + 1) * LANE)
            put(t, bscr[1, :px, lanes] + shifted(bscr[0, :px, lanes], bscr[2, :px, lanes]))
        t = main // LANE
        if rest == LANE:
            put(t, bscr[3, :px, LANE:2 * LANE] + shifted(bscr[3, :px, :LANE], bscr[3, :px, 2 * LANE:3 * LANE]))
        else:
            pair = bscr[3, :px, :LANE]
            put(t, (pltpu.roll(pair, rest, 1) + shifted(pair, bscr[3, :px, LANE:2 * LANE]))[:, :rest])

    def large_sum(m, taps, cout, acc, add=False):
        h, w, cin = m.height, m.width, m.channels
        block = 8
        blocks = h // block
        px = block * w
        main, rest = split(cout)

        def one_block(i, carry):
            b = (i + 1) % blocks

            @pl.when(i == blocks - 2)
            def _():
                receive(m, ROWS)

            lhs = packed_lhs([m.x[pl.ds(b * block + dy, block)].reshape(px, cin) for dy in range(3)], cin)
            for dx in range(3):
                bscr[dx, :px, :main] = dots(lhs, taps.columns(dx), taps.transposed)
            bscr[3, :px, :3 * rest] = dots(lhs, taps.last_columns(), taps.transposed)

            def put(t, value):
                place = (t, pl.ds(b * px, px), slice(0, value.shape[1]))
                acc[place] = value + acc[place] if add else value
            combine(px, w, cout, put)
            return carry

        lax.fori_loop(0, blocks, one_block, 0)
        receive(m, COLS)
        for side, dx, at in ((0, 0, 0), (1, 2, w - 1)):
            tscr[:h, :cout] = dots(packed_lhs(halo_slabs(m, side), cin), taps.whole(dx), taps.transposed)
            for t, lo, n in lane_tiles(cout):
                tile = acc.at[t]
                tile[pl.ds(at, h, stride=w), :] += tscr[:h, lo:lo + LANE]

    def conv_large(m, taps, cout, acc, bias, store, add=False):
        large_sum(m, taps, cout, acc, add)
        block = 8
        px = block * m.width

        def finish(b, carry):
            for t, lo, n in lane_tiles(cout):
                rows_ = pl.ds(b * px, px)
                value = jnp.maximum(acc[t, rows_, :n] + bias[lo:lo + n][None, :], 0.0)
                acc[t, rows_, :n] = value
                store(b * block, block, t, value)
            return carry

        lax.fori_loop(0, m.height // block, finish, 0)

    def conv_sum(m, taps, cout, tile_at, dys=ALL_ROWS, halo=True, add=False):
        h, w, cin = m.height, m.width, m.channels
        px = h * w
        count = px + 2 * h if halo else px
        main, rest = split(cout)
        late = [dy for dy in ALL_ROWS if dy not in dys] if halo else []
        if halo:
            receive(m, range(8))
            for side in range(2):
                for dy, part in enumerate(halo_slabs(m, side)):
                    sides[dy, side * h:(side + 1) * h, :cin] = part

        def lhs():
            def slab(dy):
                own_rows = m.x[dy:dy + h].reshape(px, cin)
                return jnp.concatenate([own_rows, sides[dy, :, :cin]], axis=0) if halo else own_rows
            return packed_lhs([slab(dy) for dy in dys], cin)

        def late_lhs():
            return packed_lhs([sides[dy, :, :cin] for dy in late], cin)

        def step(dx, carry):
            bscr[dx, :count, :main] = dots(lhs(), taps.columns(dx, dys), taps.transposed)
            if late:
                bscr[dx, px:count, :main] += dots(late_lhs(), taps.columns(dx, late), taps.transposed)
            return carry

        lax.fori_loop(0, 3, step, 0)
        bscr[3, :count, :3 * rest] = dots(lhs(), taps.last_columns(dys), taps.transposed)
        if late:
            bscr[3, px:count, :3 * rest] += dots(late_lhs(), taps.last_columns(late), taps.transposed)

        def put(t, value):
            ref, begin = tile_at(t)
            if add:
                value = value + ref[begin:begin + px, :]
            ref[begin:begin + px, :] = value
        combine(px, w, cout, put)
        if not halo:
            return
        for t, lo, n in lane_tiles(cout):
            ref, begin = tile_at(t)
            if lo < main:
                from_left, from_right = bscr[0, px:px + h, lo:lo + n], bscr[2, px + h:px + 2 * h, lo:lo + n]
            else:
                from_left, from_right = bscr[3, px:px + h, :n], bscr[3, px + h:px + 2 * h, 2 * n:3 * n]
            ref[pl.ds(begin, h, stride=w), :] += from_left
            ref[pl.ds(begin + w - 1, h, stride=w), :] += from_right

    def conv_mid(m, taps, cout, bias, store, partial=None):
        conv_sum(m, taps, cout, lambda t: (acc2.at[t], 0))
        for t, lo, n in lane_tiles(cout):
            total = acc2[t] + bias[lo:lo + n][None, :]
            if partial is not None:
                ref, first = partial(t)
                total = total + ref[first:first + h2 * w2, :]
            value = jnp.maximum(total, 0.0)
            acc2[t] = value
            store(0, h2, t, value)

    def keep_in(m, lanes=None):
        def store(first, count, t, value):
            for a, b, to in (lanes or in_order)(t, t * LANE, value.shape[1]):
                part = value[:, a:b].astype(BF16).reshape(count, m.width, b - a)
                m.x[pl.ds(1 + first, count), :, to:to + b - a] = part
        return store

    def pooled(acc, t, h, w):
        tile = acc.at[t]
        across = jnp.maximum(tile[pl.ds(0, h * w // 2, stride=2), :], tile[pl.ds(1, h * w // 2, stride=2), :])
        return across.reshape(h // 2, 2, w // 2, LANE).max(axis=1).reshape(h * w // 4, LANE)

    mx.x[1:h1 + 1] = image[...]
    acc1[0, :, :cin0] = image[...].reshape(h1 * w1, cin0).astype(F32)
    put_edges(mx, acc1)
    pl.semaphore_wait(barrier, sum(has(dr, dc).astype(jnp.int32) for dr, dc in DIRS))
    send(mx)

    for dr, dc in DIRS:
        @pl.when(jnp.logical_not(has(dr, dc)))
        def _(dr=dr, dc=dc):
            for m in maps:
                ref = m.landing(dr, dc)
                ref[...] = jnp.zeros(ref.shape, BF16)

    load("1a").wait()
    for i in range(len(biases)):
        load(i).wait()
    first = TapsFirst(stacked, stacked_rest, cin0, c1)
    depth = lax.broadcasted_iota(jnp.int32, (stacked.shape[1], cin0), 0)
    channel = lax.broadcasted_iota(jnp.int32, (stacked.shape[1], cin0), 1)
    for dx in range(3):
        total = 0.0
        for dy in range(3):
            place = jnp.where(depth == channel + dy * cin0, 1.0, 0.0).astype(BF16)
            total = total + mm(place, buf_1a[dy * 3 + dx], False)
        stacked[dx] = total.astype(BF16)
        stacked_rest[:, dx * first.rest:(dx + 1) * first.rest] = total[:, first.main:c1].astype(BF16)
    conv_large(mx, first, c1, acc1, b1a, keep_in(ma1))
    put_edges(ma1, acc1)
    send(ma1)
    load("ma0").start()
    load("ma1").start()
    load("1b").wait()
    taps = Taps(buf_a, c1, c1, rest=rest_a)
    taps.pack()
    conv_large(ma1, taps, c1, acc1, b1b, keep_in(ms1, rest_last))
    load("d1b").start()
    for t, lo, n in lane_tiles(c1):
        value = pooled(acc1, t, h1, w1)
        acc2[t] = value
        mp1.x[1:h2 + 1, :, lo:lo + n] = value[:, :n].astype(BF16).reshape(h2, w2, n)
    put_edges(mp1, acc2)
    send(mp1)
    put_edges(ms1, acc1, rest_last)
    send(ms1)
    load("mb0").start()

    load("2a").wait()
    conv_mid(mp1, Taps(buf_b, c1, c2), c2, b2a, keep_in(ma2))
    put_edges(ma2, acc2)
    send(ma2)
    load("d1a").start()
    load("d2s").start()
    load("2b").wait()
    conv_mid(ma2, Taps(buf_c, c2, c2), c2, b2b, keep_in(ms2))
    load("u2").start()

    stride = 2 * w3
    own = h3 * stride
    wide = (h3 + 2) * stride

    def at_pixel(r, c):
        return (r + 2) * stride + c + 2

    def send_small(m):
        for t, lo, n in lane_tiles(m.channels):
            tile = f3.at[t]
            lanes = slice(lo, lo + n)
            for k in range(2):
                def run(r, c, count):
                    return tile[at_pixel(r, c):at_pixel(r, c) + count, :].astype(BF16)

                def column(c):
                    return tile[pl.ds(at_pixel(0, c), h3, stride=stride), :].astype(BF16)

                m.top[k, :, lanes] = run(k, 0, w3)
                m.bottom[k, :, lanes] = run(h3 - 2 + k, 0, w3)
                m.el[k, :, lanes] = column(k)
                m.er[k, :, lanes] = column(w3 - 2 + k)
                for corner, (r, c) in enumerate(((0, 0), (0, w3 - 2), (h3 - 2, 0), (h3 - 2, w3 - 2))):
                    m.cs[corner, 2 * k:2 * k + 2, lanes] = run(r + k, c, 2)
        send(m)

    def assemble_small(m):
        receive(m, range(8))
        for t, lo, n in lane_tiles(m.channels):
            tile = f3.at[t]
            lanes = slice(lo, lo + n)
            for k in range(2):
                def put_run(r, c, value):
                    tile[at_pixel(r, c):at_pixel(r, c) + value.shape[0], :] = value.astype(F32)

                put_run(k - 2, 0, m.above[k, :, lanes])
                put_run(h3 + k, 0, m.below[k, :, lanes])
                tile[pl.ds(at_pixel(0, k - 2), h3, stride=stride), :] = m.hl[k, :, lanes].astype(F32)
                tile[pl.ds(at_pixel(0, w3 + k), h3, stride=stride), :] = m.hr[k, :, lanes].astype(F32)
                for corner, (r, c) in enumerate(((-2, -2), (-2, w3), (h3, -2), (h3, w3))):
                    put_run(r + k, c, m.cr[corner, :, lanes].astype(F32)[2 * k:2 * k + 2])
            x3[:, lanes] = tile[...].astype(BF16)

    def conv_small(src, count, cin, taps, bias, which, store):
        main, rest = split(half)

        def lhs():
            return packed_lhs([src[dy * stride:dy * stride + count, :] for dy in range(3)], cin)

        def step(dx, carry):
            bscr[dx, :count, :main] = dots(lhs(), taps.columns(dx), False)
            return carry

        lax.fori_loop(0, 3, step, 0)
        bscr[3, :count, :3 * rest] = dots(lhs(), taps.last_columns(), False)
        for t, lo, n in lane_tiles(half):
            if lo < main:
                parts = [bscr[dx, :count, lo:lo + n] for dx in range(3)]
            else:
                parts = [bscr[3, :count, dx * rest:(dx + 1) * rest] for dx in range(3)]
            value = parts[0] + pltpu.roll(parts[1], count - 1, 0) + pltpu.roll(parts[2], count - 2, 0)
            at = which * half + lo
            store(at, jnp.maximum(value + bias[at:at + n][None, :], 0.0))

    for t, lo, n in lane_tiles(c2):
        value = pooled(acc2, t, h2, w2)
        for r in range(h3):
            f3[t, at_pixel(r, 0):at_pixel(r, 0) + w3, :] = value[r * w3:(r + 1) * w3]
    send_small(mp2)
    put_edges(ms2, acc2)
    send(ms2)

    def skip_sum(t):
        return acc_skip.at[t], 0

    load("d2s").wait()
    skip_taps = Taps(buf_f, c2, c2)
    conv_sum(ms2, skip_taps, c2, skip_sum, dys=(1,), halo=False)
    load("ma0").wait()
    load("ma1").wait()
    assemble_small(mp2)

    place = lax.broadcasted_iota(jnp.int32, (wide, 1), 0)
    line, spot = place // stride, place % stride
    inside = ((line >= 1 - has(-1, 0).astype(jnp.int32)) & (line <= h3 + has(1, 0).astype(jnp.int32))
              & (spot >= 1 - has(0, -1).astype(jnp.int32)) & (spot <= w3 + has(0, 1).astype(jnp.int32)))

    def keep_padded(lo, value):
        x3b[:, lo:lo + LANE] = jnp.where(inside, value, 0.0).astype(BF16)

    def keep_flat(lo, value):
        m3[:, lo:lo + LANE] = value.astype(BF16)

    for which in range(2):
        conv_small(x3, wide, c2, Taps(buf_d, c2, half, first=9 * which), bma, which, keep_padded)
        load(("mb1", "mb2")[which]).start()
    load("mb0").wait()
    conv_small(x3b, own, c3, Taps(buf_e, c3, half, fold=2), bmb, 0, keep_flat)
    load("d2u").start()
    load("mb1").wait()
    load("mb2").wait()
    conv_small(x3b, own, c3, Taps(buf_d, c3, half, fold=2), bmb, 1, keep_flat)
    load("d2b").start()
    load("u1").start()

    load("u2").wait()
    for p in range(2):
        for q in range(2):
            at = 2 * (2 * p + q)
            value = mm(m3[...], buf_c[at:at + 2].reshape(c3, c2), False)
            for t, lo, n in lane_tiles(c2):
                bscr[0, :own, :LANE] = value[:, lo:lo + n]
                tile = acc2.at[t]
                for r in range(h3):
                    tile[pl.ds((2 * r + p) * w2 + q, w3, stride=2), :] = bscr[0, r * stride:r * stride + w3, :LANE]
    for t, lo, n in lane_tiles(c2):
        mu2.x[1:h2 + 1, :, lo:lo + n] = acc2[t].astype(BF16).reshape(h2, w2, n)
    put_edges(mu2, acc2)
    send(mu2)
    conv_sum(ms2, skip_taps, c2, skip_sum, dys=(0, 2), add=True)
    load("d2u").wait()
    conv_mid(mu2, Taps(buf_e, c2, c2), c2, bd2a, keep_in(md2), partial=skip_sum)
    put_edges(md2, acc2)
    send(md2)
    load("d1a").wait()
    large_sum(ms1, TapsT(buf_b, c1, c1, (2 * c1 - split(c1)[0], c1)), c1, acc1)
    load("d2b").wait()

    def keep_d2(begin, count, t, value):
        d2buf[:, t * LANE:(t + 1) * LANE] = value.astype(BF16)

    conv_mid(md2, Taps(buf_d, c2, c2), c2, bd2b, keep_d2)

    load("u1").wait()
    for at in range(4):
        bscr[at, :h2 * w2, :c1] = mm(d2buf[...], buf_d[9 + at // 2, (at % 2) * c1:(at % 2 + 1) * c1, :], True)
    quarter = h1 // 4
    for t, lo, n in lane_tiles(c1):
        for r in range(h2):
            tile = acc2.at[2 * r // quarter]
            for at in range(4):
                begin = (2 * r % quarter + at // 2) * w1 + at % 2
                tile[pl.ds(begin, w2, stride=2), :] = bscr[at, r * w2:(r + 1) * w2, lo:lo + LANE]
        ends = []
        for k in range(4):
            tile = acc2.at[k]
            mu1.x[1 + k * quarter:1 + (k + 1) * quarter, :, lo:lo + n] = tile[:, :n].astype(BF16).reshape(quarter, w1, n)
            left = tile[pl.ds(0, quarter, stride=w1), :]
            right = tile[pl.ds(w1 - 1, quarter, stride=w1), :]
            put_columns(mu1, slice(k * quarter, (k + 1) * quarter), left, right, in_order(t, lo, n))
            ends.append((left, right))
        (first_left, first_right), (last_left, last_right) = ends[0], ends[-1]
        put_corners(mu1, (first_left[:1], first_right[:1], last_left[quarter - 1:], last_right[quarter - 1:]),
                    in_order(t, lo, n))
    send(mu1)
    load("d1b").wait()
    taps.pack()
    conv_large(mu1, TapsT(buf_b, c1, c1, (0, split(c1)[0])), c1, acc1, bd1a, keep_in(md1), add=True)
    put_edges(md1, acc1)
    send(md1)

    def keep_last(begin, count, t, value):
        lo = t * LANE
        ma1.x[pl.ds(1 + begin, count), :, lo:lo + value.shape[1]] = value.astype(BF16).reshape(count, w1, value.shape[1])

    for d in range(8):
        @pl.when(has(*DIRS[d]))
        def _(d=d):
            remote(ma1, d).wait_send()
    conv_large(md1, taps, c1, acc1, bd1b, keep_last)

    for b in range(4):
        count = h1 // 4
        last = ma1.x[1 + b * count:1 + (b + 1) * count].reshape(count * w1, c1)
        y = mm(wh[...], last, True)
        for r in range(count):
            for o in range(wh.shape[0]):
                out[b * count + r, o:o + 1] = y[o:o + 1, r * w1:(r + 1) * w1] + bh[o]

    for m in maps:
        if m is ma1:
            continue
        for d in range(8):
            @pl.when(has(*DIRS[d]))
            def _(m=m, d=d):
                remote(m, d).wait_send()


def solution(mesh):
    rows, cols = mesh.shape["row"], mesh.shape["col"]
    tile_spec = P(("data", "row"), "col", None)

    def device_body(image, w1a, b1a, w1b, b1b, w2a, b2a, w2b, b2b, wma, bma, wmb, bmb, wu2, wd2a, bd2a, wd2b, bd2b,
                    wu1, wd1a, bd1a, wd1b, bd1b, wh, bh):
        h1, w1, cin = image.shape
        c1, c2, c3 = w1b.shape[3], w2b.shape[3], wmb.shape[3]
        couts = wh.shape[1]
        h2, w2, h3, w3 = h1 // 2, w1 // 2, h1 // 4, w1 // 4

        def stack(w):
            return w.reshape(-1, min(w.shape[2], c2), w.shape[3])

        def stack_t(w):
            return jnp.swapaxes(w, 2, 3).reshape(-1, w.shape[3], w.shape[2])

        operands = [image, w1a.reshape(9, cin, c1), b1a, stack(w1b), b1b, stack(w2a), b2a, stack(w2b), b2b,
                    stack(wma), bma, stack(wmb), bmb, stack(wu2), wd2a.reshape(9, 2 * c2, c2), bd2a, stack(wd2b), bd2b,
                    stack_t(wu1).reshape(2, 2 * c1, c2), stack_t(wd1a), bd1a, stack(wd1b), bd1b, wh.T, bh]
        in_vmem = {0, 23, 24}
        vmem = pl.BlockSpec(memory_space=pltpu.VMEM)
        hbm = pl.BlockSpec(memory_space=pl.ANY)
        nt1, nt2 = -(-c1 // LANE), c2 // LANE
        small = 2 * w3
        specs = map_specs(h1, w1, cin, c1, c2)
        scratch = (
            [shape for spec in specs for shape in map_scratch(*spec)]
            + [
                pltpu.VMEM((nt1, h1 * w1, LANE), F32), *[pltpu.VMEM((nt2, h2 * w2, LANE), F32)] * 2,
                pltpu.VMEM((4, h2 * w2 + 2 * h2, split(c2)[0]), F32), pltpu.VMEM((h1 + 16, c2), F32),
                pltpu.VMEM((3, 2 * h2, c2), BF16),
                pltpu.VMEM((nt2, (h3 + 4) * small, LANE), F32), pltpu.VMEM(((h3 + 4) * small, c2), BF16),
                pltpu.VMEM(((h3 + 2) * small, c3), BF16),
                pltpu.VMEM((h3 * small, c3), BF16), pltpu.VMEM((h2 * w2, c2), BF16),
                pltpu.VMEM((9, c1, c1), BF16), pltpu.VMEM((9, c1, c2), BF16), pltpu.VMEM((9, c2, c2), BF16),
                pltpu.VMEM((18, c2, c2), BF16), pltpu.VMEM((18, c2, c2), BF16), pltpu.VMEM((9, c2, c2), BF16),
                pltpu.VMEM((3, c1, 3 * split(c1)[1]), BF16),
                pltpu.VMEM((3, 16, c1), BF16), pltpu.VMEM((16, 3 * split(c1)[1]), BF16),
                pltpu.VMEM((9, cin, c1), BF16),
                *[pltpu.VMEM((c,), F32) for c in (c1, c1, c2, c2, c3, c3, c2, c2, c1, c1)],
                *[pltpu.SemaphoreType.DMA((len(specs), len(DIRS)))] * 2, pltpu.SemaphoreType.DMA((26,)),
            ]
        )
        y = pl.pallas_call(
            functools.partial(unet_kernel, (h1, w1, cin, c1, c2, c3, rows, cols)),
            out_shape=jax.ShapeDtypeStruct((h1, couts, w1), F32),
            in_specs=[vmem if i in in_vmem else hbm for i in range(24)] + [pl.BlockSpec(memory_space=pltpu.SMEM)],
            out_specs=vmem,
            scratch_shapes=scratch,
            compiler_params=pltpu.CompilerParams(collective_id=0, has_side_effects=True, vmem_limit_bytes=67043328),
            name="unet",
        )(*operands)
        return y.transpose(0, 2, 1)

    def program(image, *params):
        mapped = jax.shard_map(device_body, mesh=mesh, in_specs=(tile_spec,) + tuple([P()] * len(params)),
                               out_specs=tile_spec, check_vma=False)
        return mapped(image, *params)

    return program
```

profile of v0, /device:TPU:97, one launch (start us, length us, event | category | flops | bytes accessed | tf_op | source)
XLA Modules:
  0.0 74.0 jit_solution(16011081238364765237)
XLA Ops:
  0.0 1.7 %copy.26.image = bf16[32,32,4]{2,1,0:T(8,128)(2,1)} copy(bf16[32,32,4]{1,2,0:T(4,128)(2,1)} %param.25) | data formatting | bytes 16384 | tf_op args[0]
  1.7 70.8 %unet.1 = f32[32,4,32]{2,1,0:T(4,128)} custom-call(bf16[32,32,4]{2,1,0:T(8,128)(2,1)} %copy.26.image, bf16[9,4,320]{2,1,0:T(4,128)(2,1)} %bitcast.30, f32[320]{0:T(512)} %b1a_.1, bf16[9,320,320]{2,1,0:T(8,128)(2,1)} %bitcast.26, f32[320]{0:T(512)} %b1b_.1, bf16[9,320,640]{2,1,0:T(8,128)(2,1)} %bitcast.24, f32[640]{0:T(1024)} %b2a_.1, ...), custom_call_target="tpu_custom_call" | custom-call | tf_op jit(solution)/shard_map/unet/pallas_call | solution.py:714
  72.5 1.5 %copy.28 = f32[32,32,4]{1,2,0:T(4,128)} copy(f32[32,32,4]{1,2,0:T(4,128)} %bitcast.29) | data formatting | bytes 32768
where the time goes:
time: 74.2 us; the launch traced here: 74 us
  Pallas kernels  70.8 us (95%)
  local copies, waits for them, and re-layouts  3.19 us (4%)
    pallas_call x1, Pallas kernels, device_body(): pl.pallas_call(functools.partial(unet_kernel, (h1, w1, cin, c1, c2, c3, r...  70.8 us
    unnamed x2, local copies, waits for them, and re-layouts  3.19 us

commit v1 on v0

--- a/solution.py
+++ b/solution.py
@@ -207,6 +207,7 @@
         "d2b": (wd2b, buf_d.at[:9]),
         "u1": (wu1, buf_d.at[9:11]),
         "d1a": (wd1a, buf_b),
+        "d1s": (wd1a, buf_f.at[:, :c1]),
         "d1b": (wd1b, buf_a),
     }
     for i, pair in enumerate(biases):
@@ -243,6 +244,7 @@
     load("1b").start()
     load("2a").start()
     load("2b").start()
+    load("d1s").start()
 
     barrier = pltpu.get_barrier_semaphore()
     for dr, dc in DIRS:
@@ -303,7 +305,7 @@
             pair = bscr[3, :px, :LANE]
             put(t, (pltpu.roll(pair, rest, 1) + shifted(pair, bscr[3, :px, LANE:2 * LANE]))[:, :rest])
 
-    def large_sum(m, taps, cout, acc, add=False):
+    def large_sum(m, taps, cout, acc, add=False, interior=True, border=True):
         h, w, cin = m.height, m.width, m.channels
         block = 8
         blocks = h // block
@@ -328,7 +330,9 @@
             combine(px, w, cout, put)
             return carry
 
-        lax.fori_loop(0, blocks, one_block, 0)
+        lax.fori_loop(0 if interior else blocks - 2, blocks if border else blocks - 2, one_block, 0)
+        if not border:
+            return
         receive(m, COLS)
         for side, dx, at in ((0, 0, 0), (1, 2, w - 1)):
             tscr[:h, :cout] = dots(packed_lhs(halo_slabs(m, side), cin), taps.whole(dx), taps.transposed)
@@ -378,7 +382,8 @@
                 bscr[dx, px:count, :main] += dots(late_lhs(), taps.columns(dx, late), taps.transposed)
             return carry
 
-        lax.fori_loop(0, 3, step, 0)
+        for dx in range(3):
+            step(dx, 0)
         bscr[3, :count, :3 * rest] = dots(lhs(), taps.last_columns(dys), taps.transposed)
         if late:
             bscr[3, px:count, :3 * rest] += dots(late_lhs(), taps.last_columns(late), taps.transposed)
@@ -467,6 +472,9 @@
     send(mp1)
     put_edges(ms1, acc1, rest_last)
     send(ms1)
+    load("d1s").wait()
+    skip_one = TapsT(buf_f, c1, c1, (2 * c1 - split(c1)[0], c1))
+    large_sum(ms1, skip_one, c1, acc1, border=False)
     load("mb0").start()
 
     load("2a").wait()
@@ -474,6 +482,7 @@
     put_edges(ma2, acc2)
     send(ma2)
     load("d1a").start()
+    large_sum(ms1, skip_one, c1, acc1, interior=False)
     load("d2s").start()
     load("2b").wait()
     conv_mid(ma2, Taps(buf_c, c2, c2), c2, b2b, keep_in(ms2))
@@ -532,7 +541,8 @@
             bscr[dx, :count, :main] = dots(lhs(), taps.columns(dx), False)
             return carry
 
-        lax.fori_loop(0, 3, step, 0)
+        for dx in range(3):
+            step(dx, 0)
         bscr[3, :count, :3 * rest] = dots(lhs(), taps.last_columns(), False)
         for t, lo, n in lane_tiles(half):
             if lo < main:
@@ -603,8 +613,8 @@
     conv_mid(mu2, Taps(buf_e, c2, c2), c2, bd2a, keep_in(md2), partial=skip_sum)
     put_edges(md2, acc2)
     send(md2)
-    load("d1a").wait()
-    large_sum(ms1, TapsT(buf_b, c1, c1, (2 * c1 - split(c1)[0], c1)), c1, acc1)
+    load("d1b").wait()
+    taps.pack()
     load("d2b").wait()
 
     def keep_d2(begin, count, t, value):
@@ -634,8 +644,7 @@
         put_corners(mu1, (first_left[:1], first_right[:1], last_left[quarter - 1:], last_right[quarter - 1:]),
                     in_order(t, lo, n))
     send(mu1)
-    load("d1b").wait()
-    taps.pack()
+    load("d1a").wait()
     conv_large(mu1, TapsT(buf_b, c1, c1, (0, split(c1)[0])), c1, acc1, bd1a, keep_in(md1), add=True)
     put_edges(md1, acc1)
     send(md1)
@@ -708,7 +717,7 @@
                 pltpu.VMEM((3, 16, c1), BF16), pltpu.VMEM((16, 3 * split(c1)[1]), BF16),
                 pltpu.VMEM((9, cin, c1), BF16),
                 *[pltpu.VMEM((c,), F32) for c in (c1, c1, c2, c2, c3, c3, c2, c2, c1, c1)],
-                *[pltpu.SemaphoreType.DMA((len(specs), len(DIRS)))] * 2, pltpu.SemaphoreType.DMA((26,)),
+                *[pltpu.SemaphoreType.DMA((len(specs), len(DIRS)))] * 2, pltpu.SemaphoreType.DMA((27,)),
             ]
         )
         y = pl.pallas_call(

time: 74.2 us -> 69.1 us (0.931)
  Pallas kernels: 70.8 us -> 65.7 us
    pallas_call x1, Pallas kernels: 70.8 us -> 65.7 us  [device_body(): pl.pallas_call(functools.partial(unet_kernel, (h1, w1, cin, c1, c2, c3, r...]
where the time goes in v1:
time: 69.1 us; the launch traced here: 68.9 us
  Pallas kernels  65.7 us (95%)
  local copies, waits for them, and re-layouts  3.19 us (5%)
    pallas_call x1, Pallas kernels, device_body(): pl.pallas_call(functools.partial(unet_kernel, (h1, w1, cin, c1, c2, c3, r...  65.7 us
    unnamed x2, local copies, waits for them, and re-layouts  3.19 us

profile of v1, /device:TPU:97, one launch (start us, length us, event | category | flops | bytes accessed | tf_op | source)
XLA Modules:
  0.0 68.9 jit_solution(13937198734925012897)
XLA Ops:
  0.0 1.7 %copy.26.image = bf16[32,32,4]{2,1,0:T(8,128)(2,1)} copy(bf16[32,32,4]{1,2,0:T(4,128)(2,1)} %param.25) | data formatting | bytes 16384 | tf_op args[0]
  1.7 65.7 %unet.1 = f32[32,4,32]{2,1,0:T(4,128)} custom-call(bf16[32,32,4]{2,1,0:T(8,128)(2,1)} %copy.26.image, bf16[9,4,320]{2,1,0:T(4,128)(2,1)} %bitcast.30, f32[320]{0:T(512)} %b1a_.1, bf16[9,320,320]{2,1,0:T(8,128)(2,1)} %bitcast.26, f32[320]{0:T(512)} %b1b_.1, bf16[9,320,640]{2,1,0:T(8,128)(2,1)} %bitcast.24, f32[640]{0:T(1024)} %b2a_.1, ...), custom_call_target="tpu_custom_call" | custom-call | tf_op jit(solution)/shard_map/unet/pallas_call | solution.py:723
  67.5 1.5 %copy.28 = f32[32,32,4]{1,2,0:T(4,128)} copy(f32[32,32,4]{1,2,0:T(4,128)} %bitcast.29) | data formatting | bytes 32768
